TPU v7x, 128 devices: a whole 4x4x4 slice. The times are simulated.
128 devices in a mesh: row: 8 (over x, core), col: 16 (over z, y).
Axes of the slice: x: 4, y: 4, z: 4, core: 2. Of those that a mesh axis runs over, the one named last changes fastest.
Arguments:
- stored: float32 [16384, 16384], P('row', 'col'), as said below
Outputs:
- updated: float32 [16384, 16384], P('row', 'col')
- log_det: float32 [], replicated
Inputs may be any that keep to these rules, and one draw needn't show every extreme that they name: `stored`: read back into global order, the matrix is symmetric positive definite, with every eigenvalue at least 1.
All inputs are finite; a program needn't handle non-finite values.
Results may differ from a plain program's by a relative error of at most 0.0001.
Values sent between devices are 32-bit elements; how exact they have to be, the bound alone decides.
A program may use at most 256 MiB of HBM per device.

v0:
```python
import jax
import jax.numpy as jnp
from jax import lax
from jax.sharding import PartitionSpec as P

NB = 512
PANELS = 2


def from_root(value, axis, root):
    return lax.dynamic_index_in_dim(lax.all_gather(value, axis), root, 0, keepdims=False)


def from_root_2(value, axis, source):
    kept = jnp.where(lax.axis_index(axis) == source, value, 0).astype(value.dtype)
    return lax.psum(kept, axis)


def per_device(stored):
    row_count = lax.axis_size("row")
    col_count = lax.axis_size("col")
    row_index = lax.axis_index("row")
    col_index = lax.axis_index("col")
    local_rows, local_cols = stored.shape
    ratio = col_count // row_count
    col_blocks = local_cols // NB
    row_block = jnp.arange(local_rows, dtype=jnp.int32) // NB * row_count + row_index
    col_block = jnp.arange(local_cols, dtype=jnp.int32) // NB * col_count + col_index
    identity = jnp.eye(NB, dtype=jnp.float32)
    matrix = stored
    log_total = jnp.zeros((), jnp.float32)
    for number in range(PANELS):
        own_col = number // col_count
        own_row = number // row_count
        root_row = number % row_count
        root_col = number % col_count
        column_slab = matrix[:, own_col * NB : (own_col + 1) * NB]
        pivot_block = column_slab[own_row * NB : (own_row + 1) * NB]
        pivot_block = from_root(pivot_block, "row", root_row)
        factor = jnp.linalg.cholesky(pivot_block)
        inverse = jax.scipy.linalg.solve_triangular(factor, identity, lower=True)
        solved = jnp.dot(
            column_slab,
            inverse.T,
            precision=lax.Precision.HIGHEST,
            preferred_element_type=jnp.float32,
        )
        below_mask = (row_block > number)[:, None]
        at_mask = (row_block == number)[:, None]
        tiled = jnp.tile(factor, (local_rows // NB, 1))
        panel_full = jnp.where(below_mask, solved, jnp.where(at_mask, tiled, 0.0))
        log_term = 2.0 * jnp.sum(jnp.log(jnp.diagonal(factor)))
        panel_full = from_root_2(panel_full, "col", root_col)
        log_total = log_total + jnp.where(col_index == root_col, log_term, 0.0)
        picked = lax.dynamic_index_in_dim(
            panel_full.reshape(col_blocks, ratio, NB, NB), col_index // row_count, 1, keepdims=False
        )
        right_rows = from_root_2(picked.reshape(local_cols, NB), "row", col_index % row_count)
        left_rows = jnp.where(below_mask, panel_full, 0.0)
        right_rows = jnp.where((col_block > number)[:, None], right_rows, 0.0)
        matrix = matrix - jnp.dot(
            left_rows,
            right_rows.T,
            precision=lax.Precision.HIGHEST,
            preferred_element_type=jnp.float32,
        )
        old_column = matrix[:, own_col * NB : (own_col + 1) * NB]
        new_column = jnp.where(col_index == root_col, panel_full, old_column)
        matrix = matrix.at[:, own_col * NB : (own_col + 1) * NB].set(new_column)
        upper_mask = at_mask & (col_block > number)[None, :]
        matrix = jnp.where(upper_mask, 0.0, matrix)
    log_total = lax.psum(log_total, "col")
    return (matrix, log_total)


def solution(mesh):
    placed = (P("row", "col"),)
    return jax.shard_map(
        per_device, mesh=mesh, in_specs=placed, out_specs=(P("row", "col"), P()), check_vma=False
    )
```

profile of v0, /device:TPU:0, one launch (start us, length us, event | category | flops | bytes accessed | tf_op | source)
XLA Modules:
  0.0 887.8 jit_solution(12284626979522440874)
XLA Ops:
  18.9 52.1 %all-gather.5.cloned.1.call-done = f32[4096,512]{0,1:T(8,128)} async-done(((f32[512,512]{0,1:T(8,128)}), f32[4096,512]{0,1:T(8,128)}) %all-gather.5.cloned.1.call-update) | async-done | bytes 8388624 | tf_op jit(solution)/shard_map/all_gather | solution.py:11
  74.1 11.7 %cholesky.286 = f32[128,128]{1,0:T(8,128)S(1)} custom-call(f32[128,128]{1,0:T(8,128)S(1)} %cholesky.426), custom_call_target="Cholesky" | custom-call | tf_op jit(solution)/shard_map/jit(cholesky)/cholesky | solution.py:40
  85.9 9.8 %custom-call.31 = f32[1,128,128]{1,2,0:T(8,128)S(1)} custom-call(f32[1,128,128]{2,1,0:T(8,128)S(1)} %get-tuple-element.91), custom_call_target="InvertDiagBlocksLowerTriangular" | custom-call | tf_op jit(solution)/shard_map/jit(cholesky)/cholesky | solution.py:40
  98.3 11.7 %cholesky.305 = f32[128,128]{1,0:T(8,128)S(1)} custom-call(f32[128,128]{1,0:T(8,128)S(1)} %cholesky.430), custom_call_target="Cholesky" | custom-call | tf_op jit(solution)/shard_map/jit(cholesky)/cholesky | solution.py:40
  110.1 10.0 %custom-call.32 = f32[1,128,128]{1,2,0:T(8,128)S(1)} custom-call(f32[1,128,128]{2,1,0:T(8,128)S(1)} %get-tuple-element.88), custom_call_target="InvertDiagBlocksLowerTriangular" | custom-call | tf_op jit(solution)/shard_map/jit(cholesky)/cholesky | solution.py:40
  121.6 11.7 %cholesky.326 = f32[128,128]{1,0:T(8,128)S(1)} custom-call(f32[128,128]{1,0:T(8,128)S(1)} %cholesky.435), custom_call_target="Cholesky" | custom-call | tf_op jit(solution)/shard_map/jit(cholesky)/cholesky | solution.py:40
  145.3 11.7 %cholesky.343 = f32[128,128]{1,0:T(8,128)S(1)} custom-call(f32[128,128]{1,0:T(8,128)S(1)} %convolution_subtract_fusion.11), custom_call_target="Cholesky" | custom-call | tf_op jit(solution)/shard_map/jit(cholesky)/cholesky | solution.py:40
  162.6 12.0 %while.6 = (s32[]{:T(128)}, f32[512,512]{1,0:T(8,128)}, s32[4,2]{0,1:T(2,128)S(1)}, f32[4,128,128]{2,1,0:T(8,128)S(1)}, s32[]{:T(128)}) while((s32[]{:T(128)}, f32[512,512]{1,0:T(8,128)}, s32[4,2]{0,1:T(2,128)S(1)}, f32[4,128,128]{2,1,0:T(8,128)S(1)}, s32[]{:T(128)}) %tuple.69), condition=%wide.while_cond.2, body=%wide.while_body.2.sunk | while | flops 2 | bytes 131189 | solution.py:41
  174.6 39.3 %custom-call.34 = f32[4,128,128]{1,2,0:T(8,128)S(1)} custom-call(f32[4,128,128]{2,1,0:T(8,128)S(1)} %get-tuple-element.42), custom_call_target="InvertDiagBlocksLowerTriangular" | custom-call | tf_op jit(solution)/shard_map/jit(_solve_triangular)/triangular_solve | solution.py:41
  233.0 104.0 %all-reduce.6.cloned.1.call-done = f32[2048,512]{0,1:T(8,128)} async-done(((f32[2048,512]{0,1:T(8,128)}), f32[2048,512]{0,1:T(8,128)}) %all-reduce.6.cloned.1.call-update) | async-done | bytes 4194320 | tf_op jit(solution)/shard_map/psum | solution.py:16
  355.6 64.6 %all-reduce.8.cloned.1.call-done = f32[1024,512]{0,1:T(8,128)} async-done(((f32[1024,512]{0,1:T(8,128)}), f32[1024,512]{0,1:T(8,128)}) %all-reduce.8.cloned.1.call-update) | async-done | bytes 2097168 | tf_op jit(solution)/shard_map/psum | solution.py:16
  420.2 17.1 %fusion.11 = f32[2048,1024]{0,1:T(8,128)S(1)} fusion(f32[2048,1024]{0,1:T(8,128)} %copy.16, f32[2048,512]{0,1:T(8,128)} %all-reduce.6.cloned.1.call-done, f32[1024,512]{0,1:T(8,128)} %all-reduce.8.cloned.1.call-done, pred[2048]{0:T(1024)(128)(4,1)S(1)} %get-tuple-element.100, pred[1024]{0:T(1024)(128)(4,1)S(1)} %fusion.120), kind=kOutput, calls=%fused_computation.25 | convolution fusion | flops 12888571904 | bytes 23071744 | tf_op jit(solution)/shard_map/dot_general | solution.py:61
  445.3 48.9 %all-gather.7.cloned.1.call-done = f32[4096,512]{0,1:T(8,128)} async-done(((f32[512,512]{0,1:T(8,128)}), f32[4096,512]{0,1:T(8,128)}) %all-gather.7.cloned.1.call-update) | async-done | bytes 8388624 | tf_op jit(solution)/shard_map/all_gather | solution.py:11
  500.6 11.7 %cholesky.358 = f32[128,128]{1,0:T(8,128)S(1)} custom-call(f32[128,128]{1,0:T(8,128)S(1)} %cholesky.439), custom_call_target="Cholesky" | custom-call | tf_op jit(solution)/shard_map/jit(cholesky)/cholesky | solution.py:40
  525.4 11.7 %cholesky.377 = f32[128,128]{1,0:T(8,128)S(1)} custom-call(f32[128,128]{1,0:T(8,128)S(1)} %cholesky.443), custom_call_target="Cholesky" | custom-call | tf_op jit(solution)/shard_map/jit(cholesky)/cholesky | solution.py:40
  537.8 9.9 %custom-call.36 = f32[1,128,128]{1,2,0:T(8,128)S(1)} custom-call(f32[1,128,128]{2,1,0:T(8,128)S(1)} %get-tuple-element.78), custom_call_target="InvertDiagBlocksLowerTriangular" | custom-call | tf_op jit(solution)/shard_map/jit(cholesky)/cholesky | solution.py:40
  549.4 11.7 %cholesky.398 = f32[128,128]{1,0:T(8,128)S(1)} custom-call(f32[128,128]{1,0:T(8,128)S(1)} %cholesky.448), custom_call_target="Cholesky" | custom-call | tf_op jit(solution)/shard_map/jit(cholesky)/cholesky | solution.py:40
  573.0 11.7 %cholesky.415 = f32[128,128]{1,0:T(8,128)S(1)} custom-call(f32[128,128]{1,0:T(8,128)S(1)} %convolution_subtract_fusion.10), custom_call_target="Cholesky" | custom-call | tf_op jit(solution)/shard_map/jit(cholesky)/cholesky | solution.py:40
  590.8 11.5 %while.7 = (s32[]{:T(128)}, f32[512,512]{1,0:T(8,128)}, s32[4,2]{0,1:T(2,128)S(1)}, f32[4,128,128]{2,1,0:T(8,128)S(1)}, s32[]{:T(128)}) while((s32[]{:T(128)}, f32[512,512]{1,0:T(8,128)}, s32[4,2]{0,1:T(2,128)S(1)}, f32[4,128,128]{2,1,0:T(8,128)S(1)}, s32[]{:T(128)}) %tuple.87), condition=%wide.while_cond.2.clone, body=%wide.while_body.2.clone.sunk | while | flops 2 | bytes 131189 | solution.py:41
  603.0 40.1 %custom-call.38 = f32[4,128,128]{1,2,0:T(8,128)S(1)} custom-call(f32[4,128,128]{2,1,0:T(8,128)} %copy-done.8), custom_call_target="InvertDiagBlocksLowerTriangular" | custom-call | tf_op jit(solution)/shard_map/jit(_solve_triangular)/triangular_solve | solution.py:41
  661.1 103.8 %all-reduce.10.cloned.1.call-done = f32[2048,512]{0,1:T(8,128)} async-done(((f32[2048,512]{0,1:T(8,128)}), f32[2048,512]{0,1:T(8,128)}) %all-reduce.10.cloned.1.call-update) | async-done | bytes 4194320 | tf_op jit(solution)/shard_map/psum | solution.py:16
  794.3 39.1 %psum.39 = f32[]{:T(128)} all-reduce(f32[]{:T(128)S(6)} %add.143), channel_id=1, replica_groups=mesh['row'=8,'col'=16] {'col'}, use_global_device_ids=true, to_apply=%region_15.18 | all-reduce | flops 1 | bytes 8 | tf_op jit(solution)/shard_map/psum | solution.py:72
  833.4 14.9 %all-reduce.12.cloned.1.call-done = f32[1024,512]{0,1:T(8,128)} async-done(((f32[1024,512]{0,1:T(8,128)}), f32[1024,512]{0,1:T(8,128)}) %all-reduce.12.cloned.1.call-update) | async-done | bytes 2097168 | tf_op jit(solution)/shard_map/psum | solution.py:16
  848.3 17.1 %fusion.14 = f32[2048,1024]{0,1:T(8,128)S(1)} fusion(f32[2048,1024]{0,1:T(8,128)} %copy-done, f32[2048,512]{0,1:T(8,128)} %all-reduce.10.cloned.1.call-done, f32[1024,512]{0,1:T(8,128)} %all-reduce.12.cloned.1.call-done, pred[2048]{0:T(1024)(128)(4,1)S(1)} %get-tuple-element.98, pred[1024]{0:T(1024)(128)(4,1)S(1)} %fusion.121), kind=kOutput, calls=%fused_computation.26 | convolution fusion | flops 12888571904 | bytes 23071744 | tf_op jit(solution)/shard_map/dot_general | solution.py:61
  (161 shorter events, 201.8 us)
Async XLA Ops:
  7.2 63.8 %all-gather.5.cloned.1.call-start = ((), (), s32[]{:S(2)}) async-start(), calls=%async_computation.4 | async-start | bytes 9437184 | tf_op jit(solution)/shard_map/all_gather | solution.py:11
  18.7 318.3 %all-reduce.6.cloned.1.call-start = ((), (), s32[]{:S(2)}) async-start(), calls=%async_computation | async-start | bytes 8388608 | tf_op jit(solution)/shard_map/psum | solution.py:16
  74.1 11.8 %copy-start.7 = (f32[512,512]{1,0:T(8,128)}, f32[512,512]{1,0:T(8,128)S(1)}, u32[]{:S(2)}) copy-start(f32[512,512]{1,0:T(8,128)S(1)} %fusion.44) | copy-start | bytes 3145732
  215.3 6.0 copy-start.5
  219.1 4.9 slice-start.2
  222.0 2.2 slice-start.3
  232.8 187.4 %all-reduce.8.cloned.1.call-start = ((), (), s32[]{:S(2)}) async-start(), calls=%async_computation.1 | async-start | bytes 4194304 | tf_op jit(solution)/shard_map/psum | solution.py:16
  354.8 139.4 %all-gather.7.cloned.1.call-start = ((), (), s32[]{:S(2)}) async-start(), calls=%async_computation.5 | async-start | bytes 9437184 | tf_op jit(solution)/shard_map/all_gather | solution.py:11
  420.2 17.2 %copy-start.1 = (f32[2048,512]{0,1:T(8,128)S(1)}, f32[2048,512]{0,1:T(8,128)}, u32[]{:S(2)}) copy-start(f32[2048,512]{0,1:T(8,128)} %all-reduce.6.cloned.1.call-done) | copy-start | bytes 12582916
  440.2 3.4 copy-start
  444.8 320.1 %all-reduce.10.cloned.1.call-start = ((), (), s32[]{:S(2)}) async-start(), calls=%async_computation.2 | async-start | bytes 8388608 | tf_op jit(solution)/shard_map/psum | solution.py:16
  499.6 1.0 copy-start.6
  584.8 3.5 copy-start.3
  602.3 0.7 copy-start.8
  643.2 6.0 copy-start.4
  647.0 4.9 slice-start
  649.9 2.2 slice-start.1
  660.7 187.6 %all-reduce.12.cloned.1.call-start = ((), (), s32[]{:S(2)}) async-start(), calls=%async_computation.3 | async-start | bytes 4194304 | tf_op jit(solution)/shard_map/psum | solution.py:16
  848.3 17.2 %copy-start.2 = (f32[2048,512]{0,1:T(8,128)S(1)}, f32[2048,512]{0,1:T(8,128)}, u32[]{:S(2)}) copy-start(f32[2048,512]{0,1:T(8,128)} %all-reduce.10.cloned.1.call-done) | copy-start | bytes 12582916
Sparse Core Ops, SparseCore 0:
  18.9 52.0 all-gather.4
  232.9 104.0 all-reduce.5
  354.9 65.2 all-reduce.7
  444.9 49.2 all-gather.6
  660.8 104.0 all-reduce.9
  782.8 65.3 all-reduce.11
where the time goes:
time: 898 us; the launch traced here: 888 us
  waiting for transfers between devices  388 us (43%)
  other arithmetic  273 us (30%)
  local copies, waits for them, and re-layouts  90.5 us (10%)
  matrix products  74.1 us (8%)
  blocking collectives  39.1 us (4%)
  between operations  21.5 us (2%)
    psum x4, waiting for transfers between devices, from_root_2(): return lax.psum(kept, axis)  287 us
    another operation x29, other arithmetic, per_device(): factor = jnp.linalg.cholesky(pivot_block)  158 us
    all_gather x2, waiting for transfers between devices, from_root(): lax.all_gather(value, axis)  101 us
    another operation x5, other arithmetic, per_device(): inverse = jax.scipy.linalg.solve_triangular(factor, identity, lower=True)  81.7 us
    psum x1, blocking collectives, per_device(): log_total = lax.psum(log_total, 'col')  39.1 us
    dot_general x2, matrix products, per_device(): jnp.dot(left_rows, right_rows.T, precision=lax.Precision.HIGHEST, preferr...  34.3 us
    unnamed x32, local copies, waits for them, and re-layouts  31.5 us
    another operation x27, local copies, waits for them, and re-layouts, per_device(): inverse = jax.scipy.linalg.solve_triangular(factor, identity, lower=True)  23.4 us
  transfers between devices with their start and end apart: 6, of which 6 were waited for; matrix products, arithmetic and copies ran while one was open for 1% of the time, Pallas kernels for 0%

commit v1 on v0

--- a/solution.py
+++ b/solution.py
@@ -12,8 +12,12 @@
 
 
 def from_root_2(value, axis, source):
+
+    def outputs_manage(inner_x, bus_axis):
+        return jax.lax.all_gather(inner_x, bus_axis).sum(axis=0)
+
     kept = jnp.where(lax.axis_index(axis) == source, value, 0).astype(value.dtype)
-    return lax.psum(kept, axis)
+    return outputs_manage(kept, axis)
 
 
 def per_device(stored):

time: 898 us -> 1640 us (1.83)
  waiting for transfers between devices: 388 us -> 957 us
  local copies, waits for them, and re-layouts: 90.5 us -> 210 us
  other arithmetic: 273 us -> 329 us
    all_gather x0 -> x4, waiting for transfers between devices: none -> 855 us  [outputs_manage(): return jax.lax.all_gather(inner_x, bus_axis).sum(axis=0)]
    psum x4 -> x0, waiting for transfers between devices: 287 us -> none  [from_root_2(): return lax.psum(kept, axis)]
    unnamed x32, local copies, waits for them, and re-layouts: 31.5 us -> 143 us
    reduce_sum x0 -> x4, other arithmetic: none -> 65.4 us  [outputs_manage(): return jax.lax.all_gather(inner_x, bus_axis).sum(axis=0)]
where the time goes in v1:
time: 1640 us; the launch traced here: 1630 us
  waiting for transfers between devices  957 us (58%)
  other arithmetic  329 us (20%)
  local copies, waits for them, and re-layouts  210 us (13%)
  matrix products  69.2 us (4%)
  blocking collectives  39.3 us (2%)
  between operations  21.9 us (1%)
    all_gather x4, waiting for transfers between devices, outputs_manage(): return jax.lax.all_gather(inner_x, bus_axis).sum(axis=0)  855 us
    another operation x29, other arithmetic, per_device(): factor = jnp.linalg.cholesky(pivot_block)  158 us
    unnamed x32, local copies, waits for them, and re-layouts  143 us
    all_gather x2, waiting for transfers between devices, from_root(): lax.all_gather(value, axis)  102 us
    another operation x5, other arithmetic, per_device(): inverse = jax.scipy.linalg.solve_triangular(factor, identity, lower=True)  81.8 us
    reduce_sum x4, other arithmetic, outputs_manage(): return jax.lax.all_gather(inner_x, bus_axis).sum(axis=0)  65.4 us
    psum x1, blocking collectives, per_device(): log_total = lax.psum(log_total, 'col')  39.3 us
    dot_general x2, matrix products, per_device(): jnp.dot(left_rows, right_rows.T, precision=lax.Precision.HIGHEST, preferr...  33 us
  transfers between devices with their start and end apart: 6, of which 6 were waited for; matrix products, arithmetic and copies ran while one was open for 1% of the time, Pallas kernels for 0%

profile of v1, /device:TPU:0, one launch (start us, length us, event | category | flops | bytes accessed | tf_op | source)
XLA Modules:
  0.0 1628.1 jit_solution(2439249065153007164)
XLA Ops:
  18.9 52.1 %all-gather.15.cloned.1.call-done = f32[4096,512]{0,1:T(8,128)} async-done(((f32[512,512]{0,1:T(8,128)}), f32[4096,512]{0,1:T(8,128)}) %all-gather.15.cloned.1.call-update) | async-done | bytes 8388624 | tf_op jit(solution)/shard_map/all_gather | solution.py:11
  74.1 11.7 cholesky.286
  98.3 11.7 cholesky.305
  121.6 11.7 cholesky.326
  162.5 12.1 while.6
  174.6 39.3 %custom-call.34 = f32[4,128,128]{1,2,0:T(8,128)S(1)} custom-call(f32[4,128,128]{2,1,0:T(8,128)S(1)} %get-tuple-element.42), custom_call_target="InvertDiagBlocksLowerTriangular" | custom-call | tf_op jit(solution)/shard_map/jit(_solve_triangular)/triangular_solve | solution.py:45
  233.3 368.5 %all-gather.17.cloned.1.call-done = f32[32768,512]{0,1:T(8,128)} async-done(((f32[2048,512]{0,1:T(8,128)}), f32[32768,512]{0,1:T(8,128)}) %all-gather.17.cloned.1.call-update) | async-done | bytes 67108880 | tf_op jit(solution)/shard_map/all_gather | solution.py:17
  601.8 56.3 %copy.43 = f32[64,8,16,2048]{3,2,1,0:T(8,128)} copy(f32[64,8,16,2048]{3,1,2,0:T(8,128)} %bitcast.37) | data formatting | bytes 134217728
  658.1 23.3 %bitcast_reduce_fusion.1 = f32[2048,512]{0,1:T(8,128)} fusion(f32[64,8,16,2048]{3,2,1,0:T(8,128)} %copy.43), kind=kLoop, calls=%fused_computation.7 | loop fusion | flops 15728640 | bytes 71303168 | tf_op jit(solution)/shard_map/reduce_sum | solution.py:17
  697.7 83.7 %all-gather.11.cloned.1.call-done = f32[8,1024,512]{2,1,0:T(8,128)} async-done(((f32[1,1024,512]{2,1,0:T(8,128)}), f32[8,1024,512]{2,1,0:T(8,128)}) %all-gather.11.cloned.1.call-update) | async-done | bytes 16777232 | tf_op jit(solution)/shard_map/all_gather | solution.py:17
  792.8 16.5 %fusion.11 = f32[2048,1024]{0,1:T(8,128)S(1)} fusion(f32[2048,1024]{0,1:T(8,128)} %copy.28, f32[2048,512]{0,1:T(8,128)} %bitcast_reduce_fusion.1, f32[1024,512]{0,1:T(8,128)S(1)} %copy.40, pred[2048]{0:T(1024)(128)(4,1)S(1)} %get-tuple-element.102, pred[1024]{0:T(1024)(128)(4,1)S(1)} %fusion.118), kind=kOutput, calls=%fused_computation.27 | convolution fusion | flops 12888571904 | bytes 23071744 | tf_op jit(solution)/shard_map/dot_general | solution.py:65
  816.9 50.1 %all-gather.19.cloned.1.call-done = f32[4096,512]{0,1:T(8,128)} async-done(((f32[512,512]{0,1:T(8,128)}), f32[4096,512]{0,1:T(8,128)}) %all-gather.19.cloned.1.call-update) | async-done | bytes 8388624 | tf_op jit(solution)/shard_map/all_gather | solution.py:11
  870.1 11.7 cholesky.358
  893.1 11.7 cholesky.377
  916.4 11.7 cholesky.398
  939.2 11.7 cholesky.415
  955.8 12.0 while.7
  968.6 40.1 %custom-call.38 = f32[4,128,128]{1,2,0:T(8,128)S(1)} custom-call(f32[4,128,128]{2,1,0:T(8,128)} %copy-done.7), custom_call_target="InvertDiagBlocksLowerTriangular" | custom-call | tf_op jit(solution)/shard_map/jit(_solve_triangular)/triangular_solve | solution.py:45
  1026.4 368.8 %all-gather.21.cloned.1.call-done = f32[32768,512]{0,1:T(8,128)} async-done(((f32[2048,512]{0,1:T(8,128)}), f32[32768,512]{0,1:T(8,128)}) %all-gather.21.cloned.1.call-update) | async-done | bytes 67108880 | tf_op jit(solution)/shard_map/all_gather | solution.py:17
  1395.2 56.3 %copy.45 = f32[64,8,16,2048]{3,2,1,0:T(8,128)} copy(f32[64,8,16,2048]{3,1,2,0:T(8,128)} %bitcast.46) | data formatting | bytes 134217728
  1451.5 23.3 %bitcast_reduce_fusion = f32[2048,512]{0,1:T(8,128)} fusion(f32[64,8,16,2048]{3,2,1,0:T(8,128)} %copy.45), kind=kLoop, calls=%fused_computation.6 | loop fusion | flops 15728640 | bytes 71303168 | tf_op jit(solution)/shard_map/reduce_sum | solution.py:17
  1504.8 39.3 %psum.7 = f32[]{:T(128)} all-reduce(f32[]{:T(128)S(6)} %add.135), channel_id=1, replica_groups=mesh['row'=8,'col'=16] {'col'}, use_global_device_ids=true, to_apply=%region_15.18 | all-reduce | flops 1 | bytes 8 | tf_op jit(solution)/shard_map/psum | solution.py:76
  1544.1 33.7 %all-gather.13.cloned.1.call-done = f32[8,1024,512]{2,1,0:T(8,128)} async-done(((f32[1,1024,512]{2,1,0:T(8,128)}), f32[8,1024,512]{2,1,0:T(8,128)}) %all-gather.13.cloned.1.call-update) | async-done | bytes 16777232 | tf_op jit(solution)/shard_map/all_gather | solution.py:17
  1589.1 16.5 %fusion.14 = f32[2048,1024]{0,1:T(8,128)S(1)} fusion(f32[2048,1024]{0,1:T(8,128)} %copy-done, f32[2048,512]{0,1:T(8,128)} %bitcast_reduce_fusion, f32[1024,512]{0,1:T(8,128)S(1)} %copy.41, pred[2048]{0:T(1024)(128)(4,1)S(1)} %get-tuple-element.100, pred[1024]{0:T(1024)(128)(4,1)S(1)} %fusion.119), kind=kOutput, calls=%fused_computation.28 | convolution fusion | flops 12888571904 | bytes 23071744 | tf_op jit(solution)/shard_map/dot_general | solution.py:65
  (167 shorter events, 256.3 us)
Async XLA Ops:
  7.2 63.8 %all-gather.15.cloned.1.call-start = ((), (), s32[]{:S(2)}) async-start(), calls=%async_computation.2 | async-start | bytes 9437184 | tf_op jit(solution)/shard_map/all_gather | solution.py:11
  18.7 583.1 %all-gather.17.cloned.1.call-start = ((), (), s32[]{:S(2)}) async-start(), calls=%async_computation.3 | async-start | bytes 71303168 | tf_op jit(solution)/shard_map/all_gather | solution.py:17
  74.1 11.8 copy-start.6
  162.4 58.4 %copy-start.3 = (f32[512,512]{1,0:T(8,128)}, f32[512,512]{1,0:T(8,128)S(1)}, u32[]{:S(2)}) copy-start(f32[512,512]{1,0:T(8,128)S(1)} %get-tuple-element.69) | copy-start | bytes 3145732
  215.3 6.0 copy-start.5
  219.2 4.9 slice-start.2
  222.1 2.2 slice-start.3
  232.8 548.6 %all-gather.11.cloned.1.call-start = ((), (), s32[]{:S(2)}) async-start(), calls=%async_computation | async-start | bytes 18874368 | tf_op jit(solution)/shard_map/all_gather | solution.py:17
  696.8 170.1 %all-gather.19.cloned.1.call-start = ((), (), s32[]{:S(2)}) async-start(), calls=%async_computation.4 | async-start | bytes 9437184 | tf_op jit(solution)/shard_map/all_gather | solution.py:11
  792.8 16.5 %copy-start.2 = (f32[2048,512]{0,1:T(8,128)S(1)}, f32[2048,512]{0,1:T(8,128)}, u32[]{:S(2)}) copy-start(f32[2048,512]{0,1:T(8,128)} %bitcast_reduce_fusion.1) | copy-start | bytes 12582916
  812.0 3.4 copy-start
  816.6 578.6 %all-gather.21.cloned.1.call-start = ((), (), s32[]{:S(2)}) async-start(), calls=%async_computation.5 | async-start | bytes 71303168 | tf_op jit(solution)/shard_map/all_gather | solution.py:17
  967.8 0.7 copy-start.7
  1012.5 4.9 slice-start
  1015.4 2.2 slice-start.1
  1026.2 551.6 %all-gather.13.cloned.1.call-start = ((), (), s32[]{:S(2)}) async-start(), calls=%async_computation.1 | async-start | bytes 18874368 | tf_op jit(solution)/shard_map/all_gather | solution.py:17
  1487.1 6.2 copy-start.4
  1589.1 16.5 %copy-start.1 = (f32[2048,512]{0,1:T(8,128)S(1)}, f32[2048,512]{0,1:T(8,128)}, u32[]{:S(2)}) copy-start(f32[2048,512]{0,1:T(8,128)} %bitcast_reduce_fusion) | copy-start | bytes 12582916
Sparse Core Ops, SparseCore 0:
  18.9 52.0 all-gather.14
  232.9 368.8 all-gather.16
  697.0 84.4 all-gather.10
  816.7 50.2 all-gather.18
  1026.3 368.8 all-gather.20
  1493.3 84.4 all-gather.12
